TPU v7x, 32 devices: a whole 2x2x4 slice. The times are simulated.
32 devices in a mesh: grp: 2 (over core), dp: 16 (over z, y, x).
Axes of the slice: x: 2, y: 2, z: 4, core: 2. Of those that a mesh axis runs over, the one named last changes fastest.
Arguments:
- grad: bfloat16 [2, 32768, 8192], P('grp', None, 'dp'), may hold values from -40 to 40
- residual: bfloat16 [2, 32768, 8192], P('grp', None, 'dp'), may hold values from -4 to 4
- q_prev: float32 [5, 4, 8192], P(None, None, 'dp'), may hold values from -0.0625 to 0.0625
- owner_table: int32 [5], replicated, may hold values from 0 to 15, as said below
Outputs:
- new_residual: bfloat16 [2, 32768, 8192], P('grp', None, 'dp')
- q_new: float32 [5, 4, 8192], P(None, None, 'dp')
- owned: float32 [16, 4, 14336], P('dp')
Inputs may be any that keep to these rules, and one draw needn't show every extreme that they name: `owner_table`: the 5 owners are distinct.
All inputs are finite; a program needn't handle non-finite values.
Results may differ from a plain program's by a relative error of at most 0.0055.
Values sent between devices are 32-bit elements; how exact they have to be, the bound alone decides.
A program may use at most 192 MiB of HBM per device.

v0:
```python
import functools

import jax
import jax.numpy as jnp
from jax import lax
from jax.experimental import pallas as pl
from jax.experimental.pallas import tpu as pltpu
from jax.sharding import PartitionSpec as P

D = 8192
KV = 1024
FF_WIN = 14336

EPSILON = 1e-06
CHUNK = 1024
SUB = 256
SLOTS = 4
OUT_SLOTS = 4
MESH = pl.DeviceIdType.MESH
STAGES = ((3,), (4,), (0,), (1, 2))


def block_sizes():
    return [D, KV, KV, D, FF_WIN]


def block_offsets():
    offsets, at = [], 0
    for count in block_sizes():
        offsets.append(at)
        at += count
    return offsets


def piece_lanes(stage, peers):
    count = sum(block_sizes()[layer] for layer in stage)
    return -(-count // (2 * peers * 128)) * 128


def gather_kernel(peers, groups, tbl_ref, grad_ref, res_ref, q_ref, *refs):
    sizes, offsets = block_sizes(), block_offsets()
    n_chunks = grad_ref.shape[1] // CHUNK
    n_st, n_layers = len(STAGES), len(sizes)
    comp, (basis_ref, qnew_ref, owned_ref), scratch = refs[:n_layers], refs[n_layers : n_layers + 3], refs[n_layers + 3 :]
    ring, solved, qpart, qrecv = scratch[:4]
    bufs = scratch[4 : 4 + 5 * n_st]
    gsem, rsem, ssem, vsem, qssem, qrsem = scratch[4 + 5 * n_st :]
    part, sib, hs, recv, full = (bufs[i * n_st : (i + 1) * n_st] for i in range(5))
    g, d = lax.axis_index("grp"), lax.axis_index("dp")
    other = 1 - g
    rank = q_ref.shape[1]
    order = [layer for stage in STAGES for layer in stage]
    first_of, at = {}, 0
    for layer in order:
        first_of[layer] = at
        at += sizes[layer] // CHUNK

    def loads(i, layer):
        slot = lax.rem(i, SLOTS)
        local = pl.multiple_of((i - first_of[layer]) * CHUNK, CHUNK)
        at = pl.multiple_of(local + offsets[layer], CHUNK)
        return (
            pltpu.make_async_copy(grad_ref.at[0, pl.ds(at, CHUNK)], comp[layer].at[pl.ds(local, CHUNK)], gsem.at[slot]),
            pltpu.make_async_copy(res_ref.at[0, pl.ds(at, CHUNK)], ring.at[slot], rsem.at[slot]),
        )

    def spans(first, last):
        for layer in order:
            lo = max(first, first_of[layer])
            hi = min(last, first_of[layer] + sizes[layer] // CHUNK)
            if lo < hi:
                yield layer, lo, hi

    for ahead, lo, hi in spans(0, SLOTS):

        @pl.loop(lo, hi)
        def _(i):
            for copy in loads(i, ahead):
                copy.start()

    barrier = pltpu.get_barrier_semaphore()
    pl.semaphore_signal(barrier, inc=1, device_id=(other, d), device_id_type=MESH)

    @pl.loop(1, peers)
    def _(j):
        pl.semaphore_signal(barrier, inc=1, device_id=(g, lax.rem(d + j, peers)), device_id_type=MESH)

    pl.semaphore_wait(barrier, peers)

    owned_ref[...] = jnp.zeros_like(owned_ref)
    for s, stage in enumerate(STAGES):
        used = sum(sizes[layer] for layer in stage)
        if used < part[s].shape[1]:
            part[s][:, used:] = jnp.zeros((rank, part[s].shape[1] - used), jnp.float32)

    def stream(first, last, s, base, layer):
        qb = q_ref[layer].astype(jnp.bfloat16)
        col0 = base - first_of[layer] * CHUNK

        def step(i, ahead):
            for copy in loads(i, layer):
                copy.wait()
            slot = lax.rem(i, SLOTS)
            at = pl.multiple_of((i - first_of[layer]) * CHUNK, CHUNK)
            col = pl.multiple_of(col0 + i * CHUNK, CHUNK)
            for u in range(0, CHUNK, SUB):
                rng = pl.ds(at + u, SUB)
                total = comp[layer][rng, :].astype(jnp.float32) + ring[slot, u : u + SUB, :].astype(jnp.float32)
                total = total.astype(jnp.bfloat16)
                comp[layer][rng, :] = total
                part[s][:, pl.ds(col + u, SUB)] = lax.dot_general(
                    qb, total, (((1,), (1,)), ((), ())), preferred_element_type=jnp.float32
                )
            if ahead is not None:
                for copy in loads(i + SLOTS, ahead):
                    copy.start()

        for ahead, lo, hi in spans(first + SLOTS, last + SLOTS):
            pl.loop(lo - SLOTS, hi - SLOTS)(functools.partial(step, ahead=ahead))
        alone = max(first, n_chunks - SLOTS)
        if alone < last:
            pl.loop(alone, last)(functools.partial(step, ahead=None))

    def to_sibling(src, dst, s, phase):
        return pltpu.make_async_remote_copy(
            src_ref=src, dst_ref=dst, send_sem=ssem.at[s, phase], recv_sem=vsem.at[s, phase],
            device_id=(other, d), device_id_type=MESH,
        )

    def half_copy(s):
        width = sib[s].shape[1]
        src = part[s].at[:, pl.ds(pl.multiple_of(other * width, 128), width)]
        return to_sibling(src, sib[s], s, 0)

    def f0(s):
        half_copy(s).start()

    def scatter(s, j):
        to, width = lax.rem(d + j, peers), recv[s].shape[2]
        return pltpu.make_async_remote_copy(
            src_ref=hs[s].at[:, pl.ds(pl.multiple_of(to * width, 128), width)], dst_ref=recv[s].at[d],
            send_sem=ssem.at[s, 1], recv_sem=vsem.at[s, 1], device_id=(g, to), device_id_type=MESH,
        )

    def f1(s):
        half_copy(s).wait_recv()
        width, piece = sib[s].shape[1], recv[s].shape[2]
        hs[s][...] = part[s][:, pl.ds(pl.multiple_of(g * width, 128), width)] + sib[s][...]
        recv[s][d] = hs[s][:, pl.ds(pl.multiple_of(d * piece, 128), piece)]

        @pl.loop(1, peers)
        def _(j):
            scatter(s, j).start()

    def all_of(s, sem):
        ref = recv[s].at[pl.ds(0, peers - 1)]
        return pltpu.make_async_copy(ref, ref, sem)

    def my_cols(s):
        piece = recv[s].shape[2]
        return pl.ds(pl.multiple_of((g * peers + d) * piece, 128), piece)

    def f2(s):
        all_of(s, vsem.at[s, 1]).wait()
        full[s][:, my_cols(s)] = jnp.sum(recv[s][...], axis=0) / groups

        @pl.loop(1, peers)
        def _(j):
            mine = full[s].at[:, my_cols(s)]
            pltpu.make_async_remote_copy(
                src_ref=mine, dst_ref=mine, send_sem=ssem.at[s, 2], recv_sem=vsem.at[s, 2],
                device_id=(g, lax.rem(d + j, peers)), device_id_type=MESH,
            ).start()

    def full_copy(s):
        width = sib[s].shape[1]
        half = full[s].at[:, pl.ds(pl.multiple_of(g * width, 128), width)]
        return to_sibling(half, half, s, 3)

    def f3(s):
        all_of(s, vsem.at[s, 2]).wait()
        full_copy(s).start()

    def q_copy(layer):
        return pltpu.make_async_remote_copy(
            src_ref=qpart.at[layer], dst_ref=qrecv.at[layer], send_sem=qssem.at[layer], recv_sem=qrsem.at[layer],
            device_id=(other, d), device_id_type=MESH,
        )

    def f4(s):
        full_copy(s).wait_recv()
        base = 0
        for layer in STAGES[s]:
            count = sizes[layer]
            proj = full[s][:, base : base + count]
            base += count
            is_owner = jnp.where(tbl_ref[layer] == d, 1.0, 0.0).astype(jnp.float32)
            owned_ref[0, :, :count] = owned_ref[0, :, :count] + is_owner * proj
            row_id = lax.broadcasted_iota(jnp.int32, (rank, 1), 0)
            cols = []
            for i in range(rank):
                dots = jnp.sum(proj * proj[i : i + 1, :], axis=1, keepdims=True)
                cols.append(dots + jnp.where(row_id == i, EPSILON, 0.0))
            running = proj
            for k in range(rank):
                diag = jnp.sqrt(cols[k][k : k + 1, :])
                low = cols[k] / diag
                for j in range(k + 1, rank):
                    cols[j] = cols[j] - low * low[j : j + 1, :]
                row = running[k : k + 1, :] / diag
                solved[k : k + 1, :count] = row
                if k + 1 < rank:
                    running = running - low * row
            at = offsets[layer]
            basis_ref[:, at : at + count] = solved[:, :count].astype(jnp.bfloat16)
            qpart[layer] = jnp.zeros(qpart.shape[1:], jnp.float32)

            @pl.loop(0, count // CHUNK)
            def _(i):
                here = pl.multiple_of(i * CHUNK, CHUNK)
                qpart[layer] += jnp.dot(
                    basis_ref[:, pl.ds(at + here, CHUNK)], comp[layer][pl.ds(here, CHUNK), :],
                    preferred_element_type=jnp.float32,
                )

            q_copy(layer).start()

    def part_of(layer, lo, hi):
        s = [k for k, stage in enumerate(STAGES) if layer in stage][0]
        base = 0
        for before in STAGES[s]:
            if before == layer:
                break
            base += sizes[before]
        stream(first_of[layer] + lo, first_of[layer] + hi, s, base, layer)

    n = [sizes[layer] // CHUNK for layer in range(len(sizes))]
    part_of(3, 0, n[3])
    f0(0)
    part_of(4, 0, 3)
    f1(0)
    part_of(4, 3, 10)
    f2(0)
    part_of(4, 10, n[4])
    f0(1)
    part_of(0, 0, 3)
    f1(1)
    f3(0)
    part_of(0, 3, n[0])
    f0(2)
    part_of(1, 0, n[1])
    part_of(2, 0, n[2])
    f0(3)
    f1(2)
    f2(1)
    f1(3)
    f4(0)
    f2(2)
    f2(3)
    f3(1)
    f4(1)
    f3(2)
    f3(3)
    f4(2)
    f4(3)
    for s, stage in enumerate(STAGES):
        for layer in stage:
            q_copy(layer).wait()
            qnew_ref[layer] = (qpart[layer] + qrecv[layer]) / groups
    for s in range(n_st):
        half_copy(s).wait_send()
        all_of(s, ssem.at[s, 1]).wait()
        all_of(s, ssem.at[s, 2]).wait()
        full_copy(s).wait_send()


def write_kernel(basis_ref, q_ref, *refs):
    sizes, offsets = block_sizes(), block_offsets()
    comp, (out_ref, ring, sem) = refs[: len(sizes)], refs[len(sizes) :]
    n_chunks = out_ref.shape[1] // CHUNK

    def store(i):
        slot = lax.rem(i, OUT_SLOTS)
        return pltpu.make_async_copy(
            ring.at[slot], out_ref.at[0, pl.ds(pl.multiple_of(i * CHUNK, CHUNK), CHUNK)], sem.at[slot]
        )

    for layer, count in enumerate(sizes):
        q_round = q_ref[layer].astype(jnp.bfloat16)

        @pl.loop(offsets[layer] // CHUNK, (offsets[layer] + count) // CHUNK)
        def _(i):
            @pl.when(i >= OUT_SLOTS)
            def _():
                store(i - OUT_SLOTS).wait()

            slot = lax.rem(i, OUT_SLOTS)
            at = pl.multiple_of(i * CHUNK, CHUNK)
            local = pl.multiple_of(at - offsets[layer], CHUNK)
            for u in range(0, CHUNK, SUB):
                update = lax.dot_general(
                    basis_ref[:, pl.ds(at + u, SUB)], q_round, (((0,), (0,)), ((), ())),
                    preferred_element_type=jnp.float32,
                )
                left = comp[layer][pl.ds(local + u, SUB), :].astype(jnp.float32) - update
                ring[slot, u : u + SUB, :] = left.astype(jnp.bfloat16)
            store(i).start()

    @pl.loop(n_chunks - OUT_SLOTS, n_chunks)
    def _(i):
        store(i).wait()


def body(peers, groups, grad, residual, q_prev, owner_table):
    _, rows, cols = grad.shape
    layers, rank, _ = q_prev.shape
    cap = max(block_sizes())
    n_st = len(STAGES)
    piece = [piece_lanes(stage, peers) for stage in STAGES]
    f32 = jnp.float32
    vmem = pl.BlockSpec(memory_space=pltpu.VMEM)
    anyspace = pl.BlockSpec(memory_space=pl.ANY)
    *comp, basis, q_new, owned = pl.pallas_call(
        functools.partial(gather_kernel, peers, groups),
        out_shape=(
            *[pltpu.VMEM((count, cols), jnp.bfloat16) for count in block_sizes()],
            pltpu.VMEM((rank, rows), jnp.bfloat16),
            jax.ShapeDtypeStruct((layers, rank, cols), f32),
            jax.ShapeDtypeStruct((1, rank, cap), f32),
        ),
        in_specs=[pl.BlockSpec(memory_space=pltpu.SMEM), anyspace, anyspace, vmem],
        out_specs=(vmem,) * (layers + 3),
        scratch_shapes=[
            pltpu.VMEM((SLOTS, CHUNK, cols), jnp.bfloat16),
            pltpu.VMEM((rank, cap), f32),
            pltpu.VMEM((layers, rank, cols), f32),
            pltpu.VMEM((layers, rank, cols), f32),
        ]
        + [pltpu.VMEM((rank, 2 * peers * p), f32) for p in piece]
        + [pltpu.VMEM((rank, peers * p), f32) for p in piece]
        + [pltpu.VMEM((rank, peers * p), f32) for p in piece]
        + [pltpu.VMEM((peers, rank, p), f32) for p in piece]
        + [pltpu.VMEM((rank, 2 * peers * p), f32) for p in piece]
        + [
            pltpu.SemaphoreType.DMA((SLOTS,)),
            pltpu.SemaphoreType.DMA((SLOTS,)),
            pltpu.SemaphoreType.DMA((n_st, 4)),
            pltpu.SemaphoreType.DMA((n_st, 4)),
            pltpu.SemaphoreType.DMA((layers,)),
            pltpu.SemaphoreType.DMA((layers,)),
        ],
        compiler_params=pltpu.CompilerParams(
            collective_id=0, has_side_effects=True, vmem_limit_bytes=9 * 1024 * 1024
        ),
        name="stream_and_project",
    )(owner_table, grad, residual, q_prev)
    new_residual = pl.pallas_call(
        write_kernel,
        out_shape=jax.ShapeDtypeStruct((1, rows, cols), jnp.bfloat16),
        in_specs=[vmem] * (layers + 2),
        out_specs=anyspace,
        scratch_shapes=[
            pltpu.VMEM((OUT_SLOTS, CHUNK, cols), jnp.bfloat16),
            pltpu.SemaphoreType.DMA((OUT_SLOTS,)),
        ],
        compiler_params=pltpu.CompilerParams(vmem_limit_bytes=8 * 1024 * 1024),
        name="write_residual",
    )(basis, q_new, *comp)
    return new_residual, q_new, owned


def solution(mesh):
    in_specs = (P("grp", None, "dp"), P("grp", None, "dp"), P(None, None, "dp"), P())
    out_specs = (P("grp", None, "dp"), P(None, None, "dp"), P("dp", None, None))
    fn = functools.partial(body, mesh.shape["dp"], mesh.shape["grp"])
    return jax.shard_map(fn, mesh=mesh, in_specs=in_specs, out_specs=out_specs, check_vma=False)
```

profile of v0, /device:TPU:0, one launch (start us, length us, event | category | flops | bytes accessed | tf_op | source)
XLA Modules:
  0.0 65.6 jit_solution(3186867939550421551)
XLA Ops:
  0.6 0.0 copy-start
  0.6 0.8 %copy-done = f32[5,4,512]{2,1,0:T(4,128)S(1)} copy-done((f32[5,4,512]{2,1,0:T(4,128)S(1)}, f32[5,4,512]{2,1,0:T(4,128)}, u32[]{:S(2)}) %copy-start) | copy-done | bytes 40984
  1.4 0.0 copy-start.1
  1.4 0.7 copy-done.1
  2.1 46.5 %stream_and_project.1 = (bf16[8192,512]{1,0:T(8,128)(2,1)S(1)}, bf16[1024,512]{1,0:T(8,128)(2,1)S(1)}, bf16[1024,512]{1,0:T(8,128)(2,1)S(1)}, bf16[8192,512]{1,0...) custom-call(s32[5]{0:T(128)S(1)} %copy-done.1, ...), custom_call_target="tpu_custom_call" | custom-call | tf_op jit(solution)/shard_map/stream_and_project/pallas_call | solution.py:323
  48.6 15.7 %write_residual.1 = bf16[1,32768,512]{2,1,0:T(8,128)(2,1)} custom-call(bf16[4,32768]{1,0:T(4,128)(2,1)S(1)} %get-tuple-element.11.basis_ref, f32[5,4,512]{2,1,0:T(4,128)S(1)} %get-tuple-element.23.q_ref, bf16[8192,512]{1,0:T(8,128)(2,1)S(1)} %get-tuple-element.13.refs_0_, bf16[1024,512]{1,0:T(8,128)(2,1)S(1)} %get-tuple-element.14.refs_1_, ...), custom_call_target="tpu_custom_call" | custom-call | tf_op jit(solution)/shard_map/write_residual/pallas_call | solution.py:357
  64.3 0.6 copy.9
  65.0 0.7 %copy.10 = f32[1,4,14336]{2,1,0:T(4,128)} copy(f32[1,4,14336]{2,1,0:T(4,128)S(1)} %get-tuple-element.24) | data formatting | bytes 458752
Async XLA Ops:
  0.6 0.8 %copy-start = (f32[5,4,512]{2,1,0:T(4,128)S(1)}, f32[5,4,512]{2,1,0:T(4,128)}, u32[]{:S(2)}) copy-start(f32[5,4,512]{2,1,0:T(4,128)} %q_ref.1) | copy-start | bytes 122884
  1.4 0.7 copy-start.1
where the time goes:
time: 65.8 us; the launch traced here: 65.6 us
  Pallas kernels  62.3 us (95%)
  local copies, waits for them, and re-layouts  2.73 us (4%)
  between operations  0.66 us (1%)
    pallas_call x1, Pallas kernels, body(): pl.pallas_call(functools.partial(gather_kernel, peers, groups), out_shape...  46.5 us
    pallas_call x1, Pallas kernels, body(): pl.pallas_call(write_kernel, out_shape=jax.ShapeDtypeStruct((1, rows, col...  15.7 us
    unnamed x6, local copies, waits for them, and re-layouts  2.73 us

commit v1 on v0

--- a/solution.py
+++ b/solution.py
@@ -14,10 +14,14 @@
 EPSILON = 1e-06
 CHUNK = 1024
 SUB = 256
-SLOTS = 4
-OUT_SLOTS = 4
+DOT_ROWS = 4096
+SOLVE_LANES = 1024
+UPDATE_ROWS = 2048
+SLOTS = 8
+OUT_SLOTS = 6
 MESH = pl.DeviceIdType.MESH
-STAGES = ((3,), (4,), (0,), (1, 2))
+STAGES = ((4,), (3,), (0,), (1, 2))
+EARLY_LAYER, EARLY_ROWS = 4, 8192
 
 
 def block_sizes():
@@ -37,14 +41,26 @@
     return -(-count // (2 * peers * 128)) * 128
 
 
-def gather_kernel(peers, groups, tbl_ref, grad_ref, res_ref, q_ref, *refs):
+def even_split(count, most):
+    parts = -(-count // most)
+    while count % (parts * 128):
+        parts += 1
+    return count // parts
+
+
+def updated_rows(basis, q_round, comp):
+    update = lax.dot_general(basis, q_round, (((0,), (0,)), ((), ())), preferred_element_type=jnp.float32)
+    return (comp.astype(jnp.float32) - update).astype(jnp.bfloat16)
+
+
+def gather_kernel(peers, groups, grad_ref, res_ref, q_hbm, *refs):
     sizes, offsets = block_sizes(), block_offsets()
     n_chunks = grad_ref.shape[1] // CHUNK
     n_st, n_layers = len(STAGES), len(sizes)
-    comp, (basis_ref, qnew_ref, owned_ref), scratch = refs[:n_layers], refs[n_layers : n_layers + 3], refs[n_layers + 3 :]
-    ring, solved, qpart, qrecv = scratch[:4]
+    comp, (basis_ref, qnew_ref, proj_ref), scratch = refs[:n_layers], refs[n_layers : n_layers + 3], refs[n_layers + 3 :]
+    q_ref, ring, qpart, qrecv = scratch[:4]
     bufs = scratch[4 : 4 + 5 * n_st]
-    gsem, rsem, ssem, vsem, qssem, qrsem = scratch[4 + 5 * n_st :]
+    qsem, gsem, rsem, ssem, vsem, qssem, qrsem = scratch[4 + 5 * n_st :]
     part, sib, hs, recv, full = (bufs[i * n_st : (i + 1) * n_st] for i in range(5))
     g, d = lax.axis_index("grp"), lax.axis_index("dp")
     other = 1 - g
@@ -71,6 +87,8 @@
             if lo < hi:
                 yield layer, lo, hi
 
+    q_load = pltpu.make_async_copy(q_hbm, q_ref, qsem)
+    q_load.start()
     for ahead, lo, hi in spans(0, SLOTS):
 
         @pl.loop(lo, hi)
@@ -85,13 +103,12 @@
     def _(j):
         pl.semaphore_signal(barrier, inc=1, device_id=(g, lax.rem(d + j, peers)), device_id_type=MESH)
 
-    pl.semaphore_wait(barrier, peers)
-
-    owned_ref[...] = jnp.zeros_like(owned_ref)
     for s, stage in enumerate(STAGES):
         used = sum(sizes[layer] for layer in stage)
         if used < part[s].shape[1]:
             part[s][:, used:] = jnp.zeros((rank, part[s].shape[1] - used), jnp.float32)
+
+    q_load.wait()
 
     def stream(first, last, s, base, layer):
         qb = q_ref[layer].astype(jnp.bfloat16)
@@ -105,8 +122,7 @@
             col = pl.multiple_of(col0 + i * CHUNK, CHUNK)
             for u in range(0, CHUNK, SUB):
                 rng = pl.ds(at + u, SUB)
-                total = comp[layer][rng, :].astype(jnp.float32) + ring[slot, u : u + SUB, :].astype(jnp.float32)
-                total = total.astype(jnp.bfloat16)
+                total = comp[layer][rng, :] + ring[slot, u : u + SUB, :]
                 comp[layer][rng, :] = total
                 part[s][:, pl.ds(col + u, SUB)] = lax.dot_general(
                     qb, total, (((1,), (1,)), ((), ())), preferred_element_type=jnp.float32
@@ -187,43 +203,78 @@
             device_id=(other, d), device_id_type=MESH,
         )
 
+    def solve(s, base, layer):
+        count, off = sizes[layer], offsets[layer]
+        lanes = min(SOLVE_LANES, count)
+
+        def gram(i, sums):
+            sums = list(sums)
+            for v in range(0, lanes, 128):
+                cols = pl.ds(pl.multiple_of(base + i * lanes + v, 128), 128)
+                block = full[s][:, cols]
+                proj_ref[:, pl.ds(pl.multiple_of(off + i * lanes + v, 128), 128)] = block
+                for k in range(rank):
+                    sums[k] = sums[k] + block * full[s][k : k + 1, cols]
+            return tuple(sums)
+
+        sums = lax.fori_loop(0, count // lanes, gram, tuple(jnp.zeros((rank, 128), jnp.float32) for _ in range(rank)))
+        row_id = lax.broadcasted_iota(jnp.int32, (rank, 1), 0)
+        cols = [
+            jnp.sum(acc, axis=1, keepdims=True) + jnp.where(row_id == k, EPSILON, 0.0) for k, acc in enumerate(sums)
+        ]
+        lane_id = lax.broadcasted_iota(jnp.int32, (rank, 128), 1)
+        inverse = jnp.where(lane_id == lax.broadcasted_iota(jnp.int32, (rank, 128), 0), 1.0, 0.0).astype(jnp.float32)
+        for k in range(rank):
+            scale = 1.0 / jnp.sqrt(cols[k][k : k + 1, :])
+            low = cols[k] * scale
+            for j in range(k + 1, rank):
+                cols[j] = cols[j] - low * low[j : j + 1, :]
+            row = inverse[k : k + 1, :] * scale
+            below = jnp.where(row_id > k, low, 0.0)
+            inverse = jnp.where(row_id == k, row, inverse - below * row)
+        weights = [inverse[:, k : k + 1] for k in range(rank)]
+
+        @pl.loop(0, count // lanes)
+        def _(i):
+            cols = pl.ds(pl.multiple_of(base + i * lanes, 128), lanes)
+            total = weights[0] * full[s][0:1, cols]
+            for k in range(1, rank):
+                total = total + weights[k] * full[s][k : k + 1, cols]
+            basis_ref[:, pl.ds(pl.multiple_of(off + i * lanes, 128), lanes)] = total.astype(jnp.bfloat16)
+
+        rows = even_split(count, DOT_ROWS)
+
+        def dot(i, acc):
+            here = pl.multiple_of(i * rows, rows)
+            return acc + jnp.dot(
+                basis_ref[:, pl.ds(pl.multiple_of(off + here, 128), rows)], comp[layer][pl.ds(here, rows), :],
+                preferred_element_type=jnp.float32,
+            )
+
+        qpart[layer] = lax.fori_loop(0, count // rows, dot, jnp.zeros(qpart.shape[1:], jnp.float32))
+        q_copy(layer).start()
+
     def f4(s):
         full_copy(s).wait_recv()
         base = 0
         for layer in STAGES[s]:
-            count = sizes[layer]
-            proj = full[s][:, base : base + count]
-            base += count
-            is_owner = jnp.where(tbl_ref[layer] == d, 1.0, 0.0).astype(jnp.float32)
-            owned_ref[0, :, :count] = owned_ref[0, :, :count] + is_owner * proj
-            row_id = lax.broadcasted_iota(jnp.int32, (rank, 1), 0)
-            cols = []
-            for i in range(rank):
-                dots = jnp.sum(proj * proj[i : i + 1, :], axis=1, keepdims=True)
-                cols.append(dots + jnp.where(row_id == i, EPSILON, 0.0))
-            running = proj
-            for k in range(rank):
-                diag = jnp.sqrt(cols[k][k : k + 1, :])
-                low = cols[k] / diag
-                for j in range(k + 1, rank):
-                    cols[j] = cols[j] - low * low[j : j + 1, :]
-                row = running[k : k + 1, :] / diag
-                solved[k : k + 1, :count] = row
-                if k + 1 < rank:
-                    running = running - low * row
-            at = offsets[layer]
-            basis_ref[:, at : at + count] = solved[:, :count].astype(jnp.bfloat16)
-            qpart[layer] = jnp.zeros(qpart.shape[1:], jnp.float32)
-
-            @pl.loop(0, count // CHUNK)
-            def _(i):
-                here = pl.multiple_of(i * CHUNK, CHUNK)
-                qpart[layer] += jnp.dot(
-                    basis_ref[:, pl.ds(at + here, CHUNK)], comp[layer][pl.ds(here, CHUNK), :],
-                    preferred_element_type=jnp.float32,
-                )
-
-            q_copy(layer).start()
+            solve(s, base, layer)
+            base += sizes[layer]
+
+    def f5(layer):
+        q_copy(layer).wait()
+        qnew_ref[layer] = (qpart[layer] + qrecv[layer]) / groups
+
+    def f6(layer, first, last):
+        q_round = qnew_ref[layer].astype(jnp.bfloat16)
+
+        @pl.loop(first, last)
+        def _(i):
+            at = pl.multiple_of(i * UPDATE_ROWS, UPDATE_ROWS)
+            for u in range(0, UPDATE_ROWS, SUB):
+                cols = pl.ds(pl.multiple_of(offsets[layer] + at + u, 128), SUB)
+                rng = pl.ds(at + u, SUB)
+                comp[layer][rng, :] = updated_rows(basis_ref[:, cols], q_round, comp[layer][rng, :])
 
     def part_of(layer, lo, hi):
         s = [k for k, stage in enumerate(STAGES) if layer in stage][0]
@@ -235,38 +286,48 @@
         stream(first_of[layer] + lo, first_of[layer] + hi, s, base, layer)
 
     n = [sizes[layer] // CHUNK for layer in range(len(sizes))]
-    part_of(3, 0, n[3])
-    f0(0)
-    part_of(4, 0, 3)
-    f1(0)
-    part_of(4, 3, 10)
-    f2(0)
-    part_of(4, 10, n[4])
-    f0(1)
-    part_of(0, 0, 3)
-    f1(1)
-    f3(0)
-    part_of(0, 3, n[0])
-    f0(2)
-    part_of(1, 0, n[1])
-    part_of(2, 0, n[2])
-    f0(3)
-    f1(2)
-    f2(1)
-    f1(3)
-    f4(0)
-    f2(2)
-    f2(3)
-    f3(1)
-    f4(1)
-    f3(2)
-    f3(3)
-    f4(2)
-    f4(3)
-    for s, stage in enumerate(STAGES):
-        for layer in stage:
-            q_copy(layer).wait()
-            qnew_ref[layer] = (qpart[layer] + qrecv[layer]) / groups
+
+    def scoped(name, fn, *args):
+        with jax.named_scope(name):
+            fn(*args)
+
+    scoped("s4", part_of, 4, 0, n[4])
+    pl.semaphore_wait(barrier, peers)
+    scoped("f0_0", f0, 0)
+    scoped("s3a", part_of, 3, 0, 2)
+    scoped("f1_0", f1, 0)
+    scoped("s3b", part_of, 3, 2, n[3])
+    scoped("f0_1", f0, 1)
+    scoped("s0a", part_of, 0, 0, 2)
+    scoped("f1_1", f1, 1)
+    scoped("s0b", part_of, 0, 2, 5)
+    scoped("f2_0", f2, 0)
+    scoped("s0c", part_of, 0, 5, n[0])
+    scoped("f0_2", f0, 2)
+    scoped("s1", part_of, 1, 0, n[1])
+    scoped("s2", part_of, 2, 0, n[2])
+    scoped("f0_3", f0, 3)
+    scoped("f1_2", f1, 2)
+    scoped("f2_1", f2, 1)
+    scoped("f3_0", f3, 0)
+    scoped("f1_3", f1, 3)
+    scoped("f4_0", f4, 0)
+    scoped("f2_2", f2, 2)
+    scoped("f3_1", f3, 1)
+    scoped("f2_3", f2, 3)
+    scoped("f5_4", f5, 4)
+    scoped("f4_1", f4, 1)
+    scoped("f6a", f6, 4, 0, 2)
+    scoped("f3_2", f3, 2)
+    scoped("f6b", f6, 4, 2, 3)
+    scoped("f3_3", f3, 3)
+    scoped("f4_2", f4, 2)
+    scoped("f4_3", f4, 3)
+    scoped("f6c", f6, 4, 3, EARLY_ROWS // UPDATE_ROWS)
+    scoped("f5_3", f5, 3)
+    scoped("f5_0", f5, 0)
+    scoped("f5_1", f5, 1)
+    scoped("f5_2", f5, 2)
     for s in range(n_st):
         half_copy(s).wait_send()
         all_of(s, ssem.at[s, 1]).wait()
@@ -274,41 +335,77 @@
         full_copy(s).wait_send()
 
 
-def write_kernel(basis_ref, q_ref, *refs):
+def write_kernel(tbl_hbm, basis_ref, q_ref, proj_ref, *refs):
     sizes, offsets = block_sizes(), block_offsets()
-    comp, (out_ref, ring, sem) = refs[: len(sizes)], refs[len(sizes) :]
-    n_chunks = out_ref.shape[1] // CHUNK
-
-    def store(i):
+    n_layers = len(sizes)
+    comp, (out_ref, qout_ref, owned_ref), scratch = refs[:n_layers], refs[n_layers : n_layers + 3], refs[n_layers + 3 :]
+    ring, mine, table, sem, esem, tsem, qsem, osem = scratch
+    tbl_copy = pltpu.make_async_copy(tbl_hbm, table, tsem)
+    tbl_copy.start()
+
+    ready = pltpu.make_async_copy(
+        comp[EARLY_LAYER].at[pl.ds(0, EARLY_ROWS)], out_ref.at[0, pl.ds(offsets[EARLY_LAYER], EARLY_ROWS)], esem
+    )
+    ready.start()
+    q_copy = pltpu.make_async_copy(q_ref, qout_ref, qsem)
+    q_copy.start()
+
+    def store(i, at):
         slot = lax.rem(i, OUT_SLOTS)
         return pltpu.make_async_copy(
-            ring.at[slot], out_ref.at[0, pl.ds(pl.multiple_of(i * CHUNK, CHUNK), CHUNK)], sem.at[slot]
+            ring.at[slot], out_ref.at[0, pl.ds(pl.multiple_of(at, CHUNK), UPDATE_ROWS)], sem.at[slot]
         )
 
-    for layer, count in enumerate(sizes):
+    def fill(slot, into, layer, at, rows):
         q_round = q_ref[layer].astype(jnp.bfloat16)
-
-        @pl.loop(offsets[layer] // CHUNK, (offsets[layer] + count) // CHUNK)
-        def _(i):
+        for u in range(0, rows, SUB):
+            cols = pl.ds(pl.multiple_of(offsets[layer] + at + u, 128), SUB)
+            ring[slot, into + u : into + u + SUB, :] = updated_rows(
+                basis_ref[:, cols], q_round, comp[layer][pl.ds(at + u, SUB), :]
+            )
+
+    done = 0
+    for layer in (3, 0, 4):
+        first = EARLY_ROWS if layer == EARLY_LAYER else 0
+
+        @pl.loop(0, (sizes[layer] - first) // UPDATE_ROWS)
+        def _(j):
+            i = done + j
+            at = pl.multiple_of(first + j * UPDATE_ROWS, UPDATE_ROWS)
+
             @pl.when(i >= OUT_SLOTS)
             def _():
-                store(i - OUT_SLOTS).wait()
-
-            slot = lax.rem(i, OUT_SLOTS)
-            at = pl.multiple_of(i * CHUNK, CHUNK)
-            local = pl.multiple_of(at - offsets[layer], CHUNK)
-            for u in range(0, CHUNK, SUB):
-                update = lax.dot_general(
-                    basis_ref[:, pl.ds(at + u, SUB)], q_round, (((0,), (0,)), ((), ())),
-                    preferred_element_type=jnp.float32,
-                )
-                left = comp[layer][pl.ds(local + u, SUB), :].astype(jnp.float32) - update
-                ring[slot, u : u + SUB, :] = left.astype(jnp.bfloat16)
-            store(i).start()
-
-    @pl.loop(n_chunks - OUT_SLOTS, n_chunks)
+                store(i, 0).wait()
+
+            fill(lax.rem(i, OUT_SLOTS), 0, layer, at, UPDATE_ROWS)
+            store(i, offsets[layer] + at).start()
+
+        done += (sizes[layer] - first) // UPDATE_ROWS
+    store(done, 0).wait()
+    fill(done % OUT_SLOTS, 0, 1, 0, sizes[1])
+    fill(done % OUT_SLOTS, sizes[1], 2, 0, sizes[2])
+    store(done, offsets[1]).start()
+    done += 1
+
+    mine[...] = jnp.zeros_like(mine)
+    tbl_copy.wait()
+    me = lax.axis_index("dp")
+    for layer, count in enumerate(sizes):
+
+        @pl.when(table[layer] == me)
+        def _():
+            mine[0, :, :count] = proj_ref[:, offsets[layer] : offsets[layer] + count]
+
+    own_copy = pltpu.make_async_copy(mine, owned_ref, osem)
+    own_copy.start()
+
+    @pl.loop(max(0, done - OUT_SLOTS), done)
     def _(i):
-        store(i).wait()
+        store(i, 0).wait()
+
+    ready.wait()
+    q_copy.wait()
+    own_copy.wait()
 
 
 def body(peers, groups, grad, residual, q_prev, owner_table):
@@ -319,20 +416,20 @@
     piece = [piece_lanes(stage, peers) for stage in STAGES]
     f32 = jnp.float32
     vmem = pl.BlockSpec(memory_space=pltpu.VMEM)
-    anyspace = pl.BlockSpec(memory_space=pl.ANY)
-    *comp, basis, q_new, owned = pl.pallas_call(
+    hbm = pl.BlockSpec(memory_space=pltpu.HBM)
+    *comp, basis, q_new, proj = pl.pallas_call(
         functools.partial(gather_kernel, peers, groups),
         out_shape=(
             *[pltpu.VMEM((count, cols), jnp.bfloat16) for count in block_sizes()],
             pltpu.VMEM((rank, rows), jnp.bfloat16),
-            jax.ShapeDtypeStruct((layers, rank, cols), f32),
-            jax.ShapeDtypeStruct((1, rank, cap), f32),
+            pltpu.VMEM((layers, rank, cols), f32),
+            pltpu.VMEM((rank, rows), f32),
         ),
-        in_specs=[pl.BlockSpec(memory_space=pltpu.SMEM), anyspace, anyspace, vmem],
+        in_specs=[hbm, hbm, hbm],
         out_specs=(vmem,) * (layers + 3),
         scratch_shapes=[
+            pltpu.VMEM((layers, rank, cols), f32),
             pltpu.VMEM((SLOTS, CHUNK, cols), jnp.bfloat16),
-            pltpu.VMEM((rank, cap), f32),
             pltpu.VMEM((layers, rank, cols), f32),
             pltpu.VMEM((layers, rank, cols), f32),
         ]
@@ -342,6 +439,7 @@
         + [pltpu.VMEM((peers, rank, p), f32) for p in piece]
         + [pltpu.VMEM((rank, 2 * peers * p), f32) for p in piece]
         + [
+            pltpu.SemaphoreType.DMA,
             pltpu.SemaphoreType.DMA((SLOTS,)),
             pltpu.SemaphoreType.DMA((SLOTS,)),
             pltpu.SemaphoreType.DMA((n_st, 4)),
@@ -350,23 +448,33 @@
             pltpu.SemaphoreType.DMA((layers,)),
         ],
         compiler_params=pltpu.CompilerParams(
-            collective_id=0, has_side_effects=True, vmem_limit_bytes=9 * 1024 * 1024
+            collective_id=0, has_side_effects=True, vmem_limit_bytes=14 * 1024 * 1024
         ),
         name="stream_and_project",
-    )(owner_table, grad, residual, q_prev)
-    new_residual = pl.pallas_call(
+    )(grad, residual, q_prev)
+    new_residual, q_out, owned = pl.pallas_call(
         write_kernel,
-        out_shape=jax.ShapeDtypeStruct((1, rows, cols), jnp.bfloat16),
-        in_specs=[vmem] * (layers + 2),
-        out_specs=anyspace,
+        out_shape=(
+            jax.ShapeDtypeStruct((1, rows, cols), jnp.bfloat16),
+            jax.ShapeDtypeStruct((layers, rank, cols), f32),
+            jax.ShapeDtypeStruct((1, rank, cap), f32),
+        ),
+        in_specs=[hbm] + [vmem] * (layers + 3),
+        out_specs=(hbm, hbm, hbm),
         scratch_shapes=[
-            pltpu.VMEM((OUT_SLOTS, CHUNK, cols), jnp.bfloat16),
+            pltpu.VMEM((OUT_SLOTS, UPDATE_ROWS, cols), jnp.bfloat16),
+            pltpu.VMEM((1, rank, cap), f32),
+            pltpu.SMEM((layers,), jnp.int32),
             pltpu.SemaphoreType.DMA((OUT_SLOTS,)),
+            pltpu.SemaphoreType.DMA,
+            pltpu.SemaphoreType.DMA,
+            pltpu.SemaphoreType.DMA,
+            pltpu.SemaphoreType.DMA,
         ],
-        compiler_params=pltpu.CompilerParams(vmem_limit_bytes=8 * 1024 * 1024),
+        compiler_params=pltpu.CompilerParams(vmem_limit_bytes=16 * 1024 * 1024),
         name="write_residual",
-    )(basis, q_new, *comp)
-    return new_residual, q_new, owned
+    )(owner_table, basis, q_new, proj, *comp)
+    return new_residual, q_out, owned
 
 
 def solution(mesh):

time: 65.8 us -> 55.1 us (0.84)
  Pallas kernels: 62.3 us -> 53.5 us
  local copies, waits for them, and re-layouts: 2.73 us -> 0.78 us
    pallas_call x1, Pallas kernels: 15.7 us -> 11.1 us  [body(): pl.pallas_call(write_kernel, out_shape=(jax.ShapeDtypeStruct((1, rows, co...]
    pallas_call x1, Pallas kernels: 46.5 us -> 42.4 us  [body(): pl.pallas_call(functools.partial(gather_kernel, peers, groups), out_shape...]
    unnamed x6 -> x4, local copies, waits for them, and re-layouts: 2.73 us -> 0.78 us
where the time goes in v1:
time: 55.1 us; the launch traced here: 55 us
  Pallas kernels  53.5 us (97%)
  local copies, waits for them, and re-layouts  0.78 us (1%)
  between operations  0.66 us (1%)
    pallas_call x1, Pallas kernels, body(): pl.pallas_call(functools.partial(gather_kernel, peers, groups), out_shape...  42.4 us
    pallas_call x1, Pallas kernels, body(): pl.pallas_call(write_kernel, out_shape=(jax.ShapeDtypeStruct((1, rows, co...  11.1 us

profile of v1, /device:TPU:0, one launch (start us, length us, event | category | flops | bytes accessed | tf_op | source)
XLA Modules:
  0.0 55.0 jit_solution(10557949731891143340)
XLA Ops:
  0.6 0.0 copy-start
  0.6 0.8 %copy-done = f32[5,4,512]{2,1,0:T(4,128)S(1)} copy-done((f32[5,4,512]{2,1,0:T(4,128)S(1)}, f32[5,4,512]{2,1,0:T(4,128)}, u32[]{:S(2)}) %copy-start) | copy-done | bytes 40984
  1.4 0.0 copy-start.1
  1.4 42.4 %stream_and_project.1 = (bf16[8192,512]{1,0:T(8,128)(2,1)S(1)}, bf16[1024,512]{1,0:T(8,128)(2,1)S(1)}, bf16[1024,512]{1,0:T(8,128)(2,1)S(1)}, bf16[8192,512]{1,0...) custom-call(bf16[1,32768,512]{2,1,0:T(8,128)(2,1)} %grad_ref.1, ...), custom_call_target="tpu_custom_call" | custom-call | tf_op jit(solution)/shard_map/stream_and_project/pallas_call | solution.py:420
  43.8 0.0 copy-done.1
  43.8 11.1 %write_residual.1 = (bf16[1,32768,512]{2,1,0:T(8,128)(2,1)}, f32[5,4,512]{2,1,0:T(4,128)}, f32[1,4,14336]{2,1,0:T(4,128)}) custom-call(s32[5]{0:T(128)S(1)} %copy-done.1, bf16[4,32768]{1,0:T(4,128)(2,1)S(1)} %get-tuple-element.11.basis_ref, f32[5,4,512]{2,1,0:T(4,128)S(1)} %get-tuple-element.12.q_ref, f32[4,32768]{1,0:T(4,128)S(1)} %get-tuple-element.13.proj_ref, ...), custom_call_target="tpu_custom_call" | custom-call | tf_op jit(solution)/shard_map/write_residual/pallas_call | solution.py:455
Async XLA Ops:
  0.6 0.8 %copy-start = (f32[5,4,512]{2,1,0:T(4,128)S(1)}, f32[5,4,512]{2,1,0:T(4,128)}, u32[]{:S(2)}) copy-start(f32[5,4,512]{2,1,0:T(4,128)} %q_hbm.1) | copy-start | bytes 122884
  1.4 42.4 %copy-start.1 = (s32[5]{0:T(128)S(1)}, s32[5]{0:T(128)}, u32[]{:S(2)}) copy-start(s32[5]{0:T(128)} %tbl_hbm.1) | copy-start | bytes 64
